TPU v7x, 32 devices: a whole 2x2x4 slice. The times are simulated.
32 devices in a mesh: frag: 2 (over x), grid: 16 (over z, y, core).
Axes of the slice: x: 2, y: 2, z: 4, core: 2. Of those that a mesh axis runs over, the one named last changes fastest.
Arguments:
- psi: float32 [16384, 640], P(('frag', 'grid')), parts along dimension 0
- order: int32 [10], P('frag'), parts along dimension 0, may hold values from 0 to 4, each once
Outputs:
- orthonormal: float32 [16384, 640], P(('frag', 'grid')), parts along dimension 0
There are 2 independent parts, one for each index of `frag`. A program takes and returns all parts, laid end to end along the dimension named above; each array names one. Nothing has to cross between parts.
All inputs are finite; a program needn't handle non-finite values.
Results may differ from a plain program's by a relative error of at most 0.00012.
Values sent between devices are 32-bit elements; how exact they have to be, the bound alone decides.
A program may use at most 64 MiB of HBM per device.

v0:
```python
import jax
import jax.numpy as jnp
from jax import lax
from jax.sharding import PartitionSpec as P

BLOCK = 128
NBLK = 5


def contract(left, right):
    return lax.dot_general(
        left,
        right,
        (((0,), (0,)), ((), ())),
        precision=lax.Precision.HIGHEST,
        preferred_element_type=jnp.float32,
    )


def matmul(left, right):
    return jnp.dot(left, right, precision=lax.Precision.HIGHEST, preferred_element_type=jnp.float32)


def factor_inverse(gram, width):
    lower = jnp.linalg.cholesky(gram)
    return lax.linalg.triangular_solve(
        lower, jnp.eye(width, dtype=gram.dtype), left_side=True, lower=True
    )


def local(psi, order):
    scale = jnp.float32(1.0 / (psi.shape[0] * lax.axis_size("grid")))
    rows = psi.shape[0]
    reordered = jnp.take(psi.reshape(rows, NBLK, BLOCK), order, axis=1).reshape(rows, NBLK * BLOCK)
    whole = lax.psum(contract(reordered, reordered) * scale, "grid")
    inverse = factor_inverse(whole, NBLK * BLOCK)
    basis = matmul(reordered, inverse.T).reshape(rows, NBLK, BLOCK)
    result = jnp.zeros((rows, NBLK, BLOCK), psi.dtype).at[:, order, :].set(basis)
    return result.reshape(rows, NBLK * BLOCK)


def solution(mesh):
    in_specs = (P(("frag", "grid"), None), P("frag"))
    out_specs = P(("frag", "grid"), None)
    return jax.shard_map(local, mesh=mesh, in_specs=in_specs, out_specs=out_specs, check_vma=False)
```

profile of v0, /device:TPU:0, one launch (start us, length us, event | category | flops | bytes accessed | tf_op | source)
XLA Modules:
  0.0 330.1 jit_solution(3840453212950638409)
XLA Ops:
  6.5 0.7 compare_select_fusion
  7.2 0.7 compare_and_fusion
  7.9 1.7 copy.5
  10.0 0.6 gather_fusion
  10.6 1.2 select_bitcast_fusion
  11.9 1.7 copy.7
  13.6 4.5 %convolution_multiply_fusion = f32[640,640]{0,1:T(8,128)} fusion(f32[512,640]{0,1:T(8,128)S(1)} %bitcast.79), kind=kOutput, calls=%fused_computation.9 | convolution fusion | flops 2516992000 | bytes 2949120 | tf_op jit(solution)/shard_map/dot_general | solution.py:11
  18.1 0.9 iota_compare_fusion
  19.0 1.3 fusion.20
  20.2 97.1 %all-reduce.3.cloned.1.call-done = f32[640,640]{0,1:T(8,128)} async-done(((f32[640,640]{0,1:T(8,128)}), f32[640,640]{0,1:T(8,128)}) %all-reduce.3.cloned.1.call-update) | async-done | bytes 1638416 | tf_op jit(solution)/shard_map/psum | solution.py:35
  117.4 3.3 copy.9
  120.7 1.6 fusion
  122.3 1.2 copy-done.1
  123.5 11.7 %cholesky.133 = f32[128,128]{1,0:T(8,128)S(1)} custom-call(f32[128,128]{1,0:T(8,128)S(1)} %cholesky.340), custom_call_target="Cholesky" | custom-call | tf_op jit(solution)/shard_map/jit(cholesky)/cholesky | solution.py:25
  135.2 9.8 %custom-call.38 = f32[1,128,128]{1,2,0:T(8,128)S(1)} custom-call(f32[1,128,128]{2,1,0:T(8,128)S(1)} %get-tuple-element.35), custom_call_target="InvertDiagBlocksLowerTriangular" | custom-call | tf_op jit(solution)/shard_map/jit(cholesky)/cholesky | solution.py:25
  145.2 1.3 constant_dynamic-update-slice_fusion.8
  146.5 1.3 convolution_subtract_fusion.3
  147.8 11.7 %cholesky.272 = f32[128,128]{1,0:T(8,128)S(1)} custom-call(f32[128,128]{1,0:T(8,128)S(1)} %cholesky.344), custom_call_target="Cholesky" | custom-call | tf_op jit(solution)/shard_map/jit(cholesky)/cholesky | solution.py:25
  159.6 10.0 %custom-call.39 = f32[1,128,128]{1,2,0:T(8,128)S(1)} custom-call(f32[1,128,128]{2,1,0:T(8,128)S(1)} %get-tuple-element.32), custom_call_target="InvertDiagBlocksLowerTriangular" | custom-call | tf_op jit(solution)/shard_map/jit(cholesky)/cholesky | solution.py:25
  169.9 1.4 convolution_subtract_fusion.4
  171.3 11.7 %cholesky.293 = f32[128,128]{1,0:T(8,128)S(1)} custom-call(f32[128,128]{1,0:T(8,128)S(1)} %cholesky.349), custom_call_target="Cholesky" | custom-call | tf_op jit(solution)/shard_map/jit(cholesky)/cholesky | solution.py:25
  183.0 0.6 compare_reduce_fusion.2
  183.7 9.8 %custom-call.40 = f32[1,128,128]{1,2,0:T(8,128)S(1)} custom-call(f32[1,128,128]{2,1,0:T(8,128)S(1)} %get-tuple-element.29), custom_call_target="InvertDiagBlocksLowerTriangular" | custom-call | tf_op jit(solution)/shard_map/jit(cholesky)/cholesky | solution.py:25
  193.8 1.4 convolution_subtract_fusion.5
  195.2 11.9 %cholesky.312 = f32[128,128]{1,0:T(8,128)S(1)} custom-call(f32[128,128]{1,0:T(8,128)S(1)} %cholesky.354), custom_call_target="Cholesky" | custom-call | tf_op jit(solution)/shard_map/jit(cholesky)/cholesky | solution.py:25
  207.1 0.7 compare_reduce_fusion.1
  207.8 9.8 %custom-call.41 = f32[1,128,128]{1,2,0:T(8,128)S(1)} custom-call(f32[1,128,128]{2,1,0:T(8,128)S(1)} %get-tuple-element.26), custom_call_target="InvertDiagBlocksLowerTriangular" | custom-call | tf_op jit(solution)/shard_map/jit(cholesky)/cholesky | solution.py:25
  217.8 1.2 convolution_subtract_fusion.6
  219.0 11.7 %cholesky.329 = f32[128,128]{1,0:T(8,128)S(1)} custom-call(f32[128,128]{1,0:T(8,128)S(1)} %convolution_subtract_fusion.6), custom_call_target="Cholesky" | custom-call | tf_op jit(solution)/shard_map/jit(cholesky)/cholesky | solution.py:25
  230.8 0.7 compare_reduce_fusion
  231.5 0.7 compare_reduce_fusion.3
  235.2 1.3 select_select_fusion
  236.5 17.1 %while.1 = (s32[]{:T(128)}, f32[640,640]{1,0:T(8,128)}, s32[5,2]{0,1:T(2,128)S(1)}, f32[5,128,128]{2,1,0:T(8,128)}, s32[]{:T(128)}) while((s32[]{:T(128)}, f32[640,640]{1,0:T(8,128)}, s32[5,2]{0,1:T(2,128)S(1)}, f32[5,128,128]{2,1,0:T(8,128)}, s32[]{:T(128)}) %tuple.33), condition=%wide.while_cond, body=%wide.while_body.sunk | while | flops 2 | bytes 132705 | solution.py:26
  237.1 2.8 bitcast_dynamic-update-slice_fusion.2
  240.5 2.8 bitcast_dynamic-update-slice_fusion.2
  243.4 0.5 fusion.60
  244.0 2.8 bitcast_dynamic-update-slice_fusion.2
  247.4 2.8 bitcast_dynamic-update-slice_fusion.2
  250.8 2.7 bitcast_dynamic-update-slice_fusion.2
  253.6 50.3 %custom-call.42 = f32[5,128,128]{1,2,0:T(8,128)S(1)} custom-call(f32[5,128,128]{2,1,0:T(8,128)} %get-tuple-element.12), custom_call_target="InvertDiagBlocksLowerTriangular" | custom-call | tf_op jit(solution)/shard_map/triangular_solve | solution.py:26
  303.9 1.1 constant_dynamic-update-slice_fusion.3
  305.0 1.4 convolution_subtract_fusion.1
  307.0 1.4 convolution_subtract_fusion
  308.9 1.8 convolution_subtract_fusion.2
  311.1 1.9 fusion.9
  313.5 6.4 %convolution_bitcast_fusion = f32[5,512,128]{2,1,0:T(8,128)S(1)} fusion(f32[512,640,1]{0,1,2:T(8,128)S(1)} %bitcast.80, f32[5,128,640]{2,1,0:T(8,128)S(1)} %bitcast.83), kind=kOutput, calls=%fused_computation.10 | convolution fusion | flops 2516582400 | bytes 4259840 | tf_op jit(solution)/shard_map/dot_general | solution.py:21
  320.0 0.9 scatter_fusion
  321.3 1.5 copy.12
  (40 shorter events, 6.4 us)
Async XLA Ops:
  6.5 110.9 %all-reduce.3.cloned.1.call-start = ((), (), s32[]{:S(2)}) async-start(), calls=%async_computation | async-start | bytes 3276800 | tf_op jit(solution)/shard_map/psum | solution.py:35
  117.4 3.3 copy-start
  122.3 1.2 copy-start.1
  253.6 53.4 %copy-start.2 = (f32[640,640]{1,0:T(8,128)S(1)}, f32[640,640]{1,0:T(8,128)}, u32[]{:S(2)}) copy-start(f32[640,640]{1,0:T(8,128)} %fusion.20) | copy-start | bytes 4915204
Sparse Core Ops, SparseCore 0:
  18.2 99.1 all-reduce.2
where the time goes:
time: 335 us; the launch traced here: 330 us
  other arithmetic  159 us (47%)
  waiting for transfers between devices  97.2 us (29%)
  local copies, waits for them, and re-layouts  29 us (9%)
  matrix products  27.8 us (8%)
  between operations  17.2 us (5%)
    another operation x18, other arithmetic, factor_inverse(): lower = jnp.linalg.cholesky(gram)  101 us
    psum x1, waiting for transfers between devices, local(): whole = lax.psum(contract(reordered, reordered) * scale, 'grid')  97.1 us
    another operation x3, other arithmetic, factor_inverse(): lax.linalg.triangular_solve(lower, jnp.eye(width, dtype=gram.dtype), left...  51.6 us
    another operation x15, local copies, waits for them, and re-layouts  17.1 us
    another operation x9, matrix products, factor_inverse(): lax.linalg.triangular_solve(lower, jnp.eye(width, dtype=gram.dtype), left...  9.55 us
    another operation x8, matrix products, factor_inverse(): lower = jnp.linalg.cholesky(gram)  7.43 us
  transfers between devices with their start and end apart: 1, of which 1 were waited for; matrix products, arithmetic and copies ran while one was open for 1% of the time, Pallas kernels for 0%

commit v1 on v0

v1 whole, which is shorter than its diff:
```python
import functools

import jax
import jax.numpy as jnp
from jax import lax
from jax.experimental import pallas as pl
from jax.experimental.pallas import tpu as pltpu
from jax.sharding import PartitionSpec as P

BLOCK = 128
PANEL = 16
TILE = 8
HIGHEST = lax.Precision.HIGHEST


def dot(left, right, dims):
    return lax.dot_general(
        left, right, (dims, ((), ())), precision=HIGHEST, preferred_element_type=jnp.float32
    )


def pairs(count):
    return [(i, j) for i in range(count) for j in range(i, count)]


def slot(i, j, count):
    return i * count - (i * (i - 1)) // 2 + (j - i)


def gram_kernel(bits, scale, psi_ref, out_ref, part, acc, recv, full, send_sem, recv_sem):
    me = lax.axis_index("grid")
    partners = [me + (1 - 2 * ((me // 2**k) % 2)) * 2**k for k in range(bits)]
    rows = part.shape[0]
    count = psi_ref.shape[1] // BLOCK

    barrier = pltpu.get_barrier_semaphore()
    for partner in partners:
        pl.semaphore_signal(
            barrier, inc=1, device_id={"grid": partner}, device_id_type=pl.DeviceIdType.MESH
        )

    at = 0
    for i in range(count):
        left = psi_ref[:, i * BLOCK : (i + 1) * BLOCK]
        row = dot(left, psi_ref[:, i * BLOCK :], ((0,), (0,))) * scale
        for j in range(i, count):
            part[at : at + BLOCK, :] = row[:, (j - i) * BLOCK : (j - i + 1) * BLOCK]
            at += BLOCK
    if at < rows:
        part[at:, :] = jnp.zeros((rows - at, BLOCK), jnp.float32)
    pl.semaphore_wait(barrier, bits)

    def send(src, dst, index, partner):
        copy = pltpu.make_async_remote_copy(
            src_ref=src,
            dst_ref=dst,
            send_sem=send_sem.at[index],
            recv_sem=recv_sem.at[index],
            device_id={"grid": partner},
            device_id_type=pl.DeviceIdType.MESH,
        )
        copy.start()
        return copy

    offset, size, base = 0, rows, 0
    for k in range(bits):
        size //= 2
        bit = (me // 2**k) % 2
        keep = pl.multiple_of(offset + bit * size, TILE)
        give = pl.multiple_of(offset + (1 - bit) * size, TILE)
        source = part if k == 0 else acc
        landing = recv.at[pl.ds(base, size)]
        send(source.at[pl.ds(give, size)], landing, k, partners[k]).wait()
        total = source[pl.ds(keep, size), :] + recv[base : base + size, :]
        if k == bits - 1:
            full[pl.ds(keep, size), :] = total
        else:
            acc[pl.ds(keep, size), :] = total
        offset, base = keep, base + size

    for k in reversed(range(bits)):
        bit = (me // 2**k) % 2
        here = full.at[pl.ds(pl.multiple_of(offset, TILE), size)]
        send(here, here, bits + k, partners[k]).wait()
        offset = offset - bit * size
        size *= 2
    out_ref[...] = full[: out_ref.shape[0], :]


def packed_gram(psi, devices):
    points, bands = psi.shape
    count = bands // BLOCK
    used = len(pairs(count)) * BLOCK
    chunk = -(-used // (devices * TILE)) * TILE
    rows = chunk * devices
    bits = devices.bit_length() - 1
    scale = float(1.0 / (points * devices))
    return pl.pallas_call(
        functools.partial(gram_kernel, bits, scale),
        out_shape=jax.ShapeDtypeStruct((used, BLOCK), jnp.float32),
        in_specs=[pl.BlockSpec(memory_space=pltpu.VMEM)],
        out_specs=pl.BlockSpec(memory_space=pltpu.VMEM),
        scratch_shapes=[
            pltpu.VMEM((rows, BLOCK), jnp.float32),
            pltpu.VMEM((rows, BLOCK), jnp.float32),
            pltpu.VMEM((rows, BLOCK), jnp.float32),
            pltpu.VMEM((rows, BLOCK), jnp.float32),
            pltpu.SemaphoreType.DMA((2 * bits,)),
            pltpu.SemaphoreType.DMA((2 * bits,)),
        ],
        compiler_params=pltpu.CompilerParams(collective_id=0, has_side_effects=True),
    )(psi)


def factor_block(gram):
    tiles = PANEL // TILE
    row = lax.broadcasted_iota(jnp.int32, (TILE, BLOCK), 0)
    lane = lax.broadcasted_iota(jnp.int32, (TILE, BLOCK), 1)
    rest, done = gram, []
    for start in range(0, BLOCK, PANEL):
        panel = [rest[r * TILE : (r + 1) * TILE, :] for r in range(tiles)]
        columns = [
            [jnp.broadcast_to(panel[r][:, start + j : start + j + 1], (TILE, BLOCK)) for r in range(tiles)]
            for j in range(PANEL)
        ]
        inside = (lane >= start) & (lane < start + PANEL)
        panel = [
            jnp.where(inside, jnp.where(lane == row + (start + r * TILE), 1.0, 0.0), panel[r])
            for r in range(tiles)
        ]
        pivots = [jnp.ones((TILE, BLOCK), jnp.float32)] * tiles
        for j in range(PANEL):
            own, sub = divmod(j, TILE)
            pivot = jnp.broadcast_to(columns[j][own][sub : sub + 1, :], (TILE, BLOCK))
            pivots[own] = jnp.where(row == sub, pivot, pivots[own])
            if j == PANEL - 1:
                break
            inverse = 1.0 / pivot
            factors = {}
            for r in range(own, tiles):
                value = columns[j][r] * inverse
                factors[r] = jnp.where(row > sub, value, 0.0) if r == own else value
            targets = columns[j + 1 :] + [panel]
            for target in targets:
                top = jnp.broadcast_to(target[own][sub : sub + 1, :], (TILE, BLOCK))
                for r in range(own, tiles):
                    target[r] = target[r] - factors[r] * top
        norm = jnp.concatenate([panel[r] * lax.rsqrt(pivots[r]) for r in range(tiles)], axis=0)
        wide = lax.broadcasted_iota(jnp.int32, (PANEL, BLOCK), 1)
        done.append(jnp.where(wide < start + PANEL, norm, 0.0))
        left = BLOCK - start - PANEL
        if left:
            update = dot(norm, norm, ((0,), (0,)))
            wide = lax.broadcasted_iota(jnp.int32, (left, BLOCK), 1)
            inside = (wide >= start) & (wide < start + PANEL)
            rest = jnp.where(inside, 0.0, rest[PANEL:, :]) - update[start + PANEL :, :]
    return jnp.concatenate(done, axis=0)


def factor_kernel(count, order_ref, packed_ref, out_ref, work):
    def piece(s, t):
        a, b = order_ref[s], order_ref[t]
        low, high = jnp.minimum(a, b), jnp.maximum(a, b)
        at = pl.multiple_of(slot(low, high, count) * BLOCK, BLOCK)
        value = packed_ref[pl.ds(at, BLOCK), :]
        return jnp.where(a <= b, value, value.T)

    def span(i):
        return slice(i * BLOCK, (i + 1) * BLOCK)

    def put(s, t, value):
        out_ref[
            pl.ds(pl.multiple_of(order_ref[s] * BLOCK, BLOCK), BLOCK),
            pl.ds(pl.multiple_of(order_ref[t] * BLOCK, BLOCK), BLOCK),
        ] = value

    for s, t in pairs(count):
        work[span(s), span(t)] = piece(s, t)

    for s in range(count):
        inverse = factor_block(work[span(s), span(s)])
        put(s, s, inverse)
        norm = {s: inverse}
        for t in range(s + 1, count):
            norm[t] = dot(inverse, work[span(s), span(t)], ((1,), (0,)))
        for r in range(s + 1, count):
            for t in range(r, count):
                work[span(r), span(t)] -= dot(norm[r], norm[t], ((0,), (0,)))
        for t in range(s):
            norm[t] = dot(inverse, work[span(s), span(t)], ((1,), (0,)))
            put(s, t, norm[t])
            put(t, s, jnp.zeros((BLOCK, BLOCK), jnp.float32))
        for r in range(s + 1, count):
            for t in range(s + 1):
                update = dot(norm[r], norm[t], ((0,), (0,)))
                work[span(r), span(t)] = -update if t == s else work[span(r), span(t)] - update


def factor_inverse(packed, order):
    count = order.shape[0]
    bands = count * BLOCK
    return pl.pallas_call(
        functools.partial(factor_kernel, count),
        out_shape=jax.ShapeDtypeStruct((bands, bands), jnp.float32),
        in_specs=[pl.BlockSpec(memory_space=pltpu.SMEM), pl.BlockSpec(memory_space=pltpu.VMEM)],
        out_specs=pl.BlockSpec(memory_space=pltpu.VMEM),
        scratch_shapes=[pltpu.VMEM((bands, bands), jnp.float32)],
    )(order, packed)


def solution(mesh):
    devices = mesh.shape["grid"]

    def local(psi, order):
        packed = packed_gram(psi, devices)
        inverse = factor_inverse(packed, order)
        return dot(psi, inverse, ((1,), (1,)))

    in_specs = (P(("frag", "grid"), None), P("frag"))
    out_specs = P(("frag", "grid"), None)
    return jax.shard_map(local, mesh=mesh, in_specs=in_specs, out_specs=out_specs, check_vma=False)
```

time: 335 us -> 73.1 us (0.22); the launches traced: 330 us -> 72.2 us
  other arithmetic: 159 us -> 0 us
  waiting for transfers between devices: 97.2 us -> 0 us
  Pallas kernels: 0 us -> 66 us
  local copies, waits for them, and re-layouts: 29 us -> 1.47 us
  matrix products: 27.8 us -> 4.69 us
  between operations: 17.2 us -> 0.03 us
    another operation x21 -> x0, other arithmetic: 153 us -> none  [the longest x18 101 us: factor_inverse(): lower = jnp.linalg.cholesky(gram)]
    psum x1 -> x0, waiting for transfers between devices: 97.1 us -> none  [local(): whole = lax.psum(contract(reordered, reordered) * scale, 'grid')]
    pallas_call x0 -> x2, Pallas kernels: none -> 66 us  [the longest x1 38.3 us: packed_gram(): pl.pallas_call(functools.partial(gram_kernel, bits, scale), out_shape=jax...]
    another operation x21 -> x0, local copies, waits for them, and re-layouts: 17.2 us -> none
    another operation x17 -> x0, matrix products: 17 us -> none  [the longest x9 9.55 us: factor_inverse(): lax.linalg.triangular_solve(lower, jnp.eye(width, dtype=gram.dtype), left...]
    dot_general x2 -> x1, matrix products: 10.8 us -> 4.69 us  [dot(): lax.dot_general(left, right, (dims, ((), ())), precision=HIGHEST, preferr...]
  transfers between devices with their start and end apart: 1 -> 0, of which waited for: 1 -> 0; matrix products, arithmetic and copies ran while one was open for 1% -> 0% of each run, Pallas kernels for 0% -> 0%
where the time goes in v1:
time: 73.1 us; the launch traced here: 72.2 us
  Pallas kernels  66 us (90%)
  matrix products  4.69 us (6%)
  local copies, waits for them, and re-layouts  1.47 us (2%)
    pallas_call x1, Pallas kernels, packed_gram(): pl.pallas_call(functools.partial(gram_kernel, bits, scale), out_shape=jax...  38.3 us
    pallas_call x1, Pallas kernels, factor_inverse(): pl.pallas_call(functools.partial(factor_kernel, count), out_shape=jax.Sha...  27.7 us
    dot_general x1, matrix products, dot(): lax.dot_general(left, right, (dims, ((), ())), precision=HIGHEST, preferr...  4.69 us

profile of v1, /device:TPU:0, one launch (start us, length us, event | category | flops | bytes accessed | tf_op | source)
XLA Modules:
  0.0 72.2 jit_solution(10560714146399731536)
XLA Ops:
  0.0 38.3 %shard_map.28.packed_ref = f32[1920,128]{1,0:T(8,128)} custom-call(f32[512,640]{1,0:T(8,128)} %psi_ref.1), custom_call_target="tpu_custom_call" | custom-call | tf_op jit(solution)/shard_map/pallas_call | solution.py:98
  38.3 0.0 copy-start
  38.3 27.7 %shard_map.29 = f32[640,640]{1,0:T(8,128)} custom-call(s32[5]{0:T(128)} %order_ref.1, f32[1920,128]{1,0:T(8,128)} %shard_map.28.packed_ref), custom_call_target="tpu_custom_call" | custom-call | tf_op jit(solution)/shard_map/pallas_call | solution.py:202
  66.0 0.0 copy-done
  66.0 4.7 %convolution_bitcast_fusion = f32[512,640]{0,1:T(8,128)S(1)} fusion(f32[640,640]{1,0:T(8,128)} %shard_map.29, f32[512,640]{1,0:T(8,128)S(1)} %copy-done), kind=kOutput, calls=%fused_computation | convolution fusion | flops 2516582400 | bytes 4259840 | tf_op jit(solution)/shard_map/dot_general | solution.py:17
  70.7 1.5 %copy.3 = f32[512,640]{1,0:T(8,128)} copy(f32[512,640]{0,1:T(8,128)S(1)} %convolution_bitcast_fusion) | data formatting | bytes 2621440 | tf_op jit(solution)/shard_map/dot_general | solution.py:17
Async XLA Ops:
  38.3 27.7 %copy-start = (f32[512,640]{1,0:T(8,128)S(1)}, f32[512,640]{1,0:T(8,128)}, u32[]{:S(2)}) copy-start(f32[512,640]{1,0:T(8,128)} %psi_ref.1) | copy-start | bytes 3932164

commit v2 on v1

v2 whole, which is shorter than its diff:
```python
import functools

import jax
import jax.numpy as jnp
from jax import lax
from jax.experimental import pallas as pl
from jax.experimental.pallas import tpu as pltpu
from jax.sharding import PartitionSpec as P

BLOCK = 128
PANEL = 16
TILE = 8
HIGHEST = lax.Precision.HIGHEST


def dot(left, right, dims):
    return lax.dot_general(
        left, right, (dims, ((), ())), precision=HIGHEST, preferred_element_type=jnp.float32
    )


def pairs(count):
    return [(i, j) for i in range(count) for j in range(i, count)]


def slot(i, j, count):
    return i * count - (i * (i - 1)) // 2 + (j - i)


def piece_ends(count, devices):
    unit, total, ends = devices * TILE, 0, [0]
    for i in range(count):
        total += (count - i) * BLOCK
        end = -(-total // unit) * unit
        if i != count - 2 and end > ends[-1]:
            ends.append(end)
    return ends


def gram_kernel(bits, scale, ends, psi_ref, out_ref, part, acc, recv, full, send_sem, recv_sem):
    me = lax.axis_index("grid")
    digit = [(me // 2**k) % 2 for k in range(bits)]
    partners = [me + (1 - 2 * digit[k]) * 2**k for k in range(bits)]
    rows = part.shape[0]
    count = psi_ref.shape[1] // BLOCK
    pieces = len(ends) - 1
    turn = 1 + (bits - 1) // 2
    routes = [
        list(range(bits)) if p % 2 == 0 else [0, *range(turn, bits), *range(1, turn)]
        for p in range(pieces)
    ]
    offset = ends[:-1]
    size = [ends[p + 1] - ends[p] for p in range(pieces)]
    base = ends[:-1]
    copies = [None] * pieces

    barrier = pltpu.get_barrier_semaphore()
    for partner in partners:
        pl.semaphore_signal(
            barrier, inc=1, device_id={"grid": partner}, device_id_type=pl.DeviceIdType.MESH
        )

    def send(p, src, dst, step, k):
        copies[p] = pltpu.make_async_remote_copy(
            src_ref=src,
            dst_ref=dst,
            send_sem=send_sem.at[p, step],
            recv_sem=recv_sem.at[p, step],
            device_id={"grid": partners[k]},
            device_id_type=pl.DeviceIdType.MESH,
        )
        copies[p].start()

    def scatter(p, step):
        k = routes[p][step]
        half = size[p] // 2
        give = pl.multiple_of(offset[p] + (1 - digit[k]) * half, TILE)
        source = part if step == 0 else acc
        send(p, source.at[pl.ds(give, half)], recv.at[pl.ds(base[p], half)], step, k)

    def reduce(p, step):
        k = routes[p][step]
        half = size[p] // 2
        keep = pl.multiple_of(offset[p] + digit[k] * half, TILE)
        copies[p].wait()
        source = part if step == 0 else acc
        target = full if step == bits - 1 else acc
        target[pl.ds(keep, half), :] = source[pl.ds(keep, half), :] + recv[base[p] : base[p] + half, :]
        offset[p], size[p], base[p] = keep, half, base[p] + half

    def gather(p, step):
        here = full.at[pl.ds(pl.multiple_of(offset[p], TILE), size[p])]
        send(p, here, here, bits + step, routes[p][step])

    def widen(p, step):
        copies[p].wait()
        offset[p] = offset[p] - digit[routes[p][step]] * size[p]
        size[p] *= 2

    at, begun = 0, 0
    for i in range(count):
        left = psi_ref[:, i * BLOCK : (i + 1) * BLOCK]
        row = dot(left, psi_ref[:, i * BLOCK :], ((0,), (0,))) * scale
        for j in range(i, count):
            part[at : at + BLOCK, :] = row[:, (j - i) * BLOCK : (j - i + 1) * BLOCK]
            at += BLOCK
        if i == count - 1 and at < rows:
            part[at:, :] = jnp.zeros((rows - at, BLOCK), jnp.float32)
            at = rows
        if i == 0:
            pl.semaphore_wait(barrier, bits)
        while begun < pieces and ends[begun + 1] <= at:
            scatter(begun, 0)
            begun += 1

    for step in range(bits):
        for p in range(pieces):
            reduce(p, step)
            if step < bits - 1:
                scatter(p, step + 1)
            else:
                gather(p, step)
    for step in reversed(range(bits)):
        for p in range(pieces):
            widen(p, step)
            if step > 0:
                gather(p, step - 1)
    out_ref[...] = full[: out_ref.shape[0], :]


def packed_gram(psi, devices):
    points, bands = psi.shape
    count = bands // BLOCK
    used = len(pairs(count)) * BLOCK
    ends = piece_ends(count, devices)
    bits = devices.bit_length() - 1
    scale = float(1.0 / (points * devices))
    buffer = pltpu.VMEM((ends[-1], BLOCK), jnp.float32)
    semaphores = pltpu.SemaphoreType.DMA((len(ends) - 1, 2 * bits))
    return pl.pallas_call(
        functools.partial(gram_kernel, bits, scale, ends),
        out_shape=jax.ShapeDtypeStruct((used, BLOCK), jnp.float32),
        in_specs=[pl.BlockSpec(memory_space=pltpu.VMEM)],
        out_specs=pl.BlockSpec(memory_space=pltpu.VMEM),
        scratch_shapes=[buffer, buffer, buffer, buffer, semaphores, semaphores],
        compiler_params=pltpu.CompilerParams(collective_id=0, has_side_effects=True),
    )(psi)


def factor_block(gram):
    tiles = PANEL // TILE
    row = lax.broadcasted_iota(jnp.int32, (TILE, BLOCK), 0)
    lane = lax.broadcasted_iota(jnp.int32, (TILE, BLOCK), 1)
    rest, done = gram, []
    for start in range(0, BLOCK, PANEL):
        panel = [rest[r * TILE : (r + 1) * TILE, :] for r in range(tiles)]
        columns = [
            [jnp.broadcast_to(panel[r][:, start + j : start + j + 1], (TILE, BLOCK)) for r in range(tiles)]
            for j in range(PANEL)
        ]
        inside = (lane >= start) & (lane < start + PANEL)
        panel = [
            jnp.where(inside, jnp.where(lane == row + (start + r * TILE), 1.0, 0.0), panel[r])
            for r in range(tiles)
        ]
        pivots = [jnp.ones((TILE, BLOCK), jnp.float32)] * tiles
        for j in range(PANEL):
            own, sub = divmod(j, TILE)
            pivot = jnp.broadcast_to(columns[j][own][sub : sub + 1, :], (TILE, BLOCK))
            pivots[own] = jnp.where(row == sub, pivot, pivots[own])
            if j == PANEL - 1:
                break
            inverse = 1.0 / pivot
            factors = {}
            for r in range(own, tiles):
                value = columns[j][r] * inverse
                factors[r] = jnp.where(row > sub, value, 0.0) if r == own else value
            targets = columns[j + 1 :] + [panel]
            for target in targets:
                top = jnp.broadcast_to(target[own][sub : sub + 1, :], (TILE, BLOCK))
                for r in range(own, tiles):
                    target[r] = target[r] - factors[r] * top
        norm = jnp.concatenate([panel[r] * lax.rsqrt(pivots[r]) for r in range(tiles)], axis=0)
        wide = lax.broadcasted_iota(jnp.int32, (PANEL, BLOCK), 1)
        done.append(jnp.where(wide < start + PANEL, norm, 0.0))
        left = BLOCK - start - PANEL
        if left:
            update = dot(norm, norm, ((0,), (0,)))
            wide = lax.broadcasted_iota(jnp.int32, (left, BLOCK), 1)
            inside = (wide >= start) & (wide < start + PANEL)
            rest = jnp.where(inside, 0.0, rest[PANEL:, :]) - update[start + PANEL :, :]
    return jnp.concatenate(done, axis=0)


def factor_kernel(count, order_ref, packed_ref, psi_ref, out_ref, work, x):
    def piece(s, t):
        a, b = order_ref[s], order_ref[t]
        low, high = jnp.minimum(a, b), jnp.maximum(a, b)
        at = pl.multiple_of(slot(low, high, count) * BLOCK, BLOCK)
        value = packed_ref[pl.ds(at, BLOCK), :]
        return jnp.where(a <= b, value, value.T)

    def span(i):
        return slice(i * BLOCK, (i + 1) * BLOCK)

    def home(s):
        return pl.ds(pl.multiple_of(order_ref[s] * BLOCK, BLOCK), BLOCK)

    for s, t in pairs(count):
        work[span(s), span(t)] = piece(s, t)
    for s in range(count):
        x[:, span(s)] = psi_ref[:, home(s)]

    for s in range(count):
        inverse = factor_block(work[span(s), span(s)])
        if s < count - 1:
            after = (s + 1) * BLOCK
            norm = dot(inverse, work[span(s), after:], ((1,), (0,)))
            for r in range(s + 1, count):
                skip = r * BLOCK - after
                left = norm[:, skip : skip + BLOCK]
                work[span(r), r * BLOCK :] -= dot(left, norm[:, skip:], ((0,), (0,)))
        q = dot(x[:, span(s)], inverse, ((1,), (1,)))
        out_ref[:, home(s)] = q
        if s < count - 1:
            x[:, after:] -= dot(q, norm, ((1,), (0,)))


def orthonormalize(packed, psi, order):
    count = order.shape[0]
    rows, bands = psi.shape
    vmem = pl.BlockSpec(memory_space=pltpu.VMEM)
    return pl.pallas_call(
        functools.partial(factor_kernel, count),
        out_shape=jax.ShapeDtypeStruct((rows, bands), jnp.float32),
        in_specs=[pl.BlockSpec(memory_space=pltpu.SMEM), vmem, vmem],
        out_specs=vmem,
        scratch_shapes=[
            pltpu.VMEM((bands, bands), jnp.float32),
            pltpu.VMEM((rows, bands), jnp.float32),
        ],
    )(order, packed, psi)


def solution(mesh):
    devices = mesh.shape["grid"]

    def local(psi, order):
        return orthonormalize(packed_gram(psi, devices), psi, order)

    in_specs = (P(("frag", "grid"), None), P("frag"))
    out_specs = P(("frag", "grid"), None)
    return jax.shard_map(local, mesh=mesh, in_specs=in_specs, out_specs=out_specs, check_vma=False)
```

time: 73.1 us -> 63.1 us (0.86); the launches traced: 72.2 us -> 63 us
  matrix products: 4.69 us -> 0 us
  Pallas kernels: 66 us -> 62.9 us
  local copies, waits for them, and re-layouts: 1.47 us -> 0 us
    dot_general x1 -> x0, matrix products: 4.69 us -> none  [dot(): lax.dot_general(left, right, (dims, ((), ())), precision=HIGHEST, preferr...]
    pallas_call x2, Pallas kernels: 66 us -> 62.9 us  [the longest x1 33.1 us: packed_gram(): pl.pallas_call(functools.partial(gram_kernel, bits, scale, ends), out_sha...]
    dot_general x1 -> x0, local copies, waits for them, and re-layouts: 1.46 us -> none  [dot(): lax.dot_general(left, right, (dims, ((), ())), precision=HIGHEST, preferr...]
where the time goes in v2:
time: 63.1 us; the launch traced here: 63 us
  Pallas kernels  62.9 us (100%)
    pallas_call x1, Pallas kernels, packed_gram(): pl.pallas_call(functools.partial(gram_kernel, bits, scale, ends), out_sha...  33.1 us
    pallas_call x1, Pallas kernels, orthonormalize(): pl.pallas_call(functools.partial(factor_kernel, count), out_shape=jax.Sha...  29.9 us

profile of v2, /device:TPU:0, one launch (start us, length us, event | category | flops | bytes accessed | tf_op | source)
XLA Modules:
  0.0 63.0 jit_solution(6957934053279215465)
XLA Ops:
  0.0 33.1 %shard_map.28.packed_ref = f32[1920,128]{1,0:T(8,128)} custom-call(f32[512,640]{1,0:T(8,128)} %psi_ref.3), custom_call_target="tpu_custom_call" | custom-call | tf_op jit(solution)/shard_map/pallas_call | solution.py:140
  33.1 29.9 %shard_map.29 = f32[512,640]{1,0:T(8,128)} custom-call(s32[5]{0:T(128)} %order_ref.1, f32[1920,128]{1,0:T(8,128)} %shard_map.28.packed_ref, f32[512,640]{1,0:T(8,128)} %psi_ref.3), custom_call_target="tpu_custom_call" | custom-call | tf_op jit(solution)/shard_map/pallas_call | solution.py:233

commit v3 on v2

--- a/solution.py
+++ b/solution.py
@@ -145,6 +145,13 @@
         scratch_shapes=[buffer, buffer, buffer, buffer, semaphores, semaphores],
         compiler_params=pltpu.CompilerParams(collective_id=0, has_side_effects=True),
     )(psi)
+
+
+def thirds(value):
+    high = value.astype(jnp.bfloat16)
+    value = value - high.astype(jnp.float32)
+    middle = value.astype(jnp.bfloat16)
+    return high, middle, (value - middle.astype(jnp.float32)).astype(jnp.bfloat16)
 
 
 def factor_block(gram):
@@ -185,10 +192,22 @@
         done.append(jnp.where(wide < start + PANEL, norm, 0.0))
         left = BLOCK - start - PANEL
         if left:
-            update = dot(norm, norm, ((0,), (0,)))
+            high, middle, low = thirds(norm)
+            left_parts = jnp.concatenate([low, high, middle, middle, high, high], axis=0)
+            right_parts = jnp.concatenate([high, low, middle, high, middle, high], axis=0)
+            turned = left_parts.T
+            cuts = [start + PANEL, start + 2 * PANEL, BLOCK]
+            update = jnp.concatenate(
+                [
+                    jnp.dot(turned[a:b, :], right_parts, preferred_element_type=jnp.float32)
+                    for a, b in zip(cuts, cuts[1:])
+                    if a < b
+                ],
+                axis=0,
+            )
             wide = lax.broadcasted_iota(jnp.int32, (left, BLOCK), 1)
             inside = (wide >= start) & (wide < start + PANEL)
-            rest = jnp.where(inside, 0.0, rest[PANEL:, :]) - update[start + PANEL :, :]
+            rest = jnp.where(inside, 0.0, rest[PANEL:, :]) - update
     return jnp.concatenate(done, axis=0)
 
 

time: 63.1 us -> 58.5 us (0.927)
  Pallas kernels: 62.9 us -> 58.3 us
    pallas_call x1, Pallas kernels: 29.9 us -> 25.2 us  [orthonormalize(): pl.pallas_call(functools.partial(factor_kernel, count), out_shape=jax.Sha...]
where the time goes in v3:
time: 58.5 us; the launch traced here: 58.3 us
  Pallas kernels  58.3 us (100%)
    pallas_call x1, Pallas kernels, packed_gram(): pl.pallas_call(functools.partial(gram_kernel, bits, scale, ends), out_sha...  33.1 us
    pallas_call x1, Pallas kernels, orthonormalize(): pl.pallas_call(functools.partial(factor_kernel, count), out_shape=jax.Sha...  25.2 us

profile of v3, /device:TPU:0, one launch (start us, length us, event | category | flops | bytes accessed | tf_op | source)
XLA Modules:
  0.0 58.3 jit_solution(14881465838904320498)
XLA Ops:
  0.0 33.1 %shard_map.28.packed_ref = f32[1920,128]{1,0:T(8,128)} custom-call(f32[512,640]{1,0:T(8,128)} %psi_ref.3), custom_call_target="tpu_custom_call" | custom-call | tf_op jit(solution)/shard_map/pallas_call | solution.py:140
  33.1 25.2 %shard_map.29 = f32[512,640]{1,0:T(8,128)} custom-call(s32[5]{0:T(128)} %order_ref.1, f32[1920,128]{1,0:T(8,128)} %shard_map.28.packed_ref, f32[512,640]{1,0:T(8,128)} %psi_ref.3), custom_call_target="tpu_custom_call" | custom-call | tf_op jit(solution)/shard_map/pallas_call | solution.py:252
